TPU v7x, 32 devices: a whole 2x2x4 slice. The times are simulated.
32 devices in a mesh: seq: 8 (over z, y), head: 4 (over x, core).
Axes of the slice: x: 2, y: 2, z: 4, core: 2. Of those that a mesh axis runs over, the one named last changes fastest.
Arguments:
- query: bfloat16 [128, 32, 128], P(None, 'head'), may hold values from -8 to 8
- key_cache: bfloat16 [16384, 16, 128], P('seq', 'head'), may hold values from -6 to 6
- value_cache: bfloat16 [16384, 16, 128], P('seq', 'head'), may hold values from -6 to 6
- lengths: int32 [8], P('seq'), may hold values from 1 to 2048, 12288 in all
- out_weight: bfloat16 [4608, 4096], P('seq', 'head'), may hold values from -10 to 10
- norm_gain: float32 [4608], P('seq'), may hold values from 0.1 to 1.9
Outputs:
- normed: bfloat16 [128, 4608], P(None, 'seq')
Inputs may be any that keep to these rules, and one draw needn't show every extreme that they name: `lengths`: every block has at least one valid position, and some block is valid throughout.
All inputs are finite; a program needn't handle non-finite values.
Results may differ from a plain program's by a relative error of at most 0.0083.
Values may be sent and summed in bfloat16 or wider, within the bound.
A program may use at most 128 MiB of HBM per device.

v0:
```python
import jax
import jax.numpy as jnp
from jax import lax
from jax.sharding import PartitionSpec as P

D = 4608
QPRE = 144


def merged(value, axis, join):
    pieces = jax.tree.map(lambda part: lax.all_gather(part, axis), value)
    head = jax.tree.map(lambda part: part[0], pieces)
    tail = jax.tree.map(lambda part: part[1:], pieces)
    so_far, _ = lax.scan(lambda so_far, share: (join(so_far, share), None), head, tail)
    return so_far


def combine_partials(former, latter):
    max_former, sum_former, acc_former = former
    max_latter, sum_latter, acc_latter = latter
    new_max = jnp.maximum(max_former, max_latter)
    factor_former = jnp.exp(max_former - new_max)
    factor_latter = jnp.exp(max_latter - new_max)
    new_sum = factor_former * sum_former + factor_latter * sum_latter
    new_acc = factor_former[..., None] * acc_former + factor_latter[..., None] * acc_latter
    return (new_max, new_sum, new_acc)


def body(query, key_cache, value_cache, lengths, out_weight, norm_gain):
    tok_count, heads_local, head_dim = query.shape
    key_count, kv_local, unused_dim = key_cache.shape
    group_size = heads_local // kv_local
    score_scale = float(QPRE) ** (-0.5)
    grouped = query.reshape(tok_count, kv_local, group_size, head_dim)
    scores = (
        jnp.einsum("tkgd,ckd->kgtc", grouped, key_cache, preferred_element_type=jnp.float32)
        * score_scale
    )
    inside = lax.iota(jnp.int32, key_count) < lengths[0]
    scores = jnp.where(inside, scores, jnp.float32(-1e30))
    block_max = jnp.max(scores, axis=-1)
    weights = jnp.where(inside, jnp.exp(scores - block_max[..., None]), jnp.float32(0.0))
    block_sum = jnp.sum(weights, axis=-1)
    weights_low = weights.astype(jnp.bfloat16)
    weighted = jnp.einsum(
        "kgtc,ckd->tkgd", weights_low, value_cache, preferred_element_type=jnp.float32
    )
    weighted = weighted.reshape(tok_count, heads_local, head_dim)
    block_max = jnp.transpose(block_max, (2, 0, 1)).reshape(tok_count, heads_local)
    block_sum = jnp.transpose(block_sum, (2, 0, 1)).reshape(tok_count, heads_local)
    peak_all, total_all, combined = merged(
        (block_max, block_sum, weighted), "seq", combine_partials
    )
    attention = (
        (combined / total_all[..., None])
        .reshape(tok_count, heads_local * head_dim)
        .astype(jnp.bfloat16)
    )
    projected_part = lax.dot_general(
        attention, out_weight, (((1,), (1,)), ((), ())), preferred_element_type=jnp.float32
    )
    projected = lax.psum(projected_part, "head")
    square_part = jnp.sum(projected * projected, axis=-1)
    square_total = lax.psum(square_part, "seq")
    mean_square = square_total / D
    normed = projected * lax.rsqrt(mean_square + 1e-06)[:, None] * norm_gain[None, :]
    return normed.astype(jnp.bfloat16)


def solution(mesh):
    placed = (
        P(None, "head", None),
        P("seq", "head", None),
        P("seq", "head", None),
        P("seq"),
        P("seq", "head"),
        P("seq"),
    )
    return jax.shard_map(
        body, mesh=mesh, in_specs=placed, out_specs=P(None, "seq"), check_vma=False
    )
```

profile of v0, /device:TPU:0, one launch (start us, length us, event | category | flops | bytes accessed | tf_op | source)
XLA Modules:
  0.0 174.1 jit_solution(1487944032741304655)
XLA Ops:
  7.4 3.9 %bitcast_reduce_fusion = (f32[4,2,128]{2,1,0:T(2,128)S(1)}, f32[4,2048,128,2]{2,1,3,0:T(8,128)S(1)}) fusion(pred[2048]{0:T(1024)(128)(4,1)S(1)} %iota_compare_fusion, bf16[128,4,2,128]{3,2,1,0:T(2,128)(2,1)} %bitcast.62, bf16[2048,4,128,1]{2,1,0,3:T(4,128)(2,1)} %bitcast.61), kind=kOutput, calls=%fused_computation.9 | convolution fusion | flops 543161344 | bytes 10754048 | tf_op jit(solution)/shard_map/tkgd,ckd->kgtc/dot_general | solution.py:36
  11.2 3.4 %fusion.7 = f32[4,2,128,128]{3,2,1,0:T(8,128)S(1)} fusion(f32[4,2048,128,2]{2,1,3,0:T(8,128)S(1)} %get-tuple-element.64, f32[4,2,128]{2,1,0:T(2,128)S(1)} %get-tuple-element.63, pred[2048]{0:T(1024)(128)(4,1)S(1)} %iota_compare_fusion, bf16[2048,4,128,1]{2,1,0,3:T(4,128)(2,1)S(1)} %bitcast.56), kind=kOutput, calls=%fused_computation.15 | convolution fusion | flops 547356672 | bytes 11016192 | tf_op jit(solution)/shard_map/kgtc,ckd->tkgd/dot_general | solution.py:45
  14.7 1.1 copy.21
  15.9 4.6 %fusion.6 = f32[4,2,128]{2,1,0:T(2,128)S(1)} fusion(f32[4,2048,128,2]{2,1,3,0:T(8,128)} %copy-done.1, f32[4,2,128]{2,1,0:T(2,128)S(1)} %get-tuple-element.63, pred[2048]{0:T(1024)(128)(4,1)S(1)} %iota_compare_fusion), kind=kLoop, calls=%fused_computation.14 | loop fusion | flops 10484736 | bytes 8398848 | tf_op jit(solution)/shard_map/reduce_sum | solution.py:43
  20.5 33.0 %all_gather.10 = f32[8,128,8]{1,2,0:T(8,128)S(1)} all-gather(f32[1,128,8]{1,2,0:T(8,128)S(1)} %bitcast.60), channel_id=1, replica_groups=mesh['seq'=8,'head'=4] {'seq'}, dimensions={0}, use_global_device_ids=true | all-gather | bytes 36864 | tf_op jit(solution)/shard_map/all_gather | solution.py:11
  53.5 31.8 %all_gather.9 = f32[8,128,8]{1,2,0:T(8,128)S(1)} all-gather(f32[1,128,8]{1,2,0:T(8,128)S(1)} %bitcast.59), channel_id=1, replica_groups=mesh['seq'=8,'head'=4] {'seq'}, dimensions={0}, use_global_device_ids=true | all-gather | bytes 36864 | tf_op jit(solution)/shard_map/all_gather | solution.py:11
  85.3 6.9 %all-gather.2.cloned.1.call-done = f32[8,128,8,128]{3,2,1,0:T(8,128)} async-done(((f32[1,128,8,128]{3,2,1,0:T(8,128)}), f32[8,128,8,128]{3,2,1,0:T(8,128)}) %all-gather.2.cloned.1.call-update) | async-done | bytes 4194320 | tf_op jit(solution)/shard_map/all_gather | solution.py:11
  92.2 1.1 slice_bitcast_fusion
  93.3 4.1 %slice.29 = f32[7,128,8,128]{3,2,1,0:T(8,128)} slice(f32[8,128,8,128]{3,2,1,0:T(8,128)} %all-gather.2.cloned.1.call-done), slice={[1:8], [0:128], [0:8], [0:128]} | slice | bytes 7340032 | tf_op jit(solution)/shard_map/slice | solution.py:13
  97.4 11.7 %while.14 = (s32[]{:T(128)}, f32[128,8]{0,1:T(8,128)S(1)}, f32[128,8]{0,1:T(8,128)S(1)}, f32[128,8,128]{2,1,0:T(8,128)S(1)}, f32[7,128,8]{1,2,0:T(8,128)S(1)}, /...) while((s32[]{:T(128)}, f32[128,8]{0,1:T(8,128)S(1)}, f32[128,8]{0,1:T(8,128)S(1)}, ...), condition=%wide.region_3.4_spmd, body=%wide.region_2.3_spmd.sunk | while | flops 399362 | bytes 1630309 | solution.py:14
  97.4 0.1 copy.47
  97.6 1.4 fusion.26
  99.1 0.1 copy.47
  99.2 0.1 copy.48
  99.3 1.4 fusion.26
  100.7 0.1 copy.47
  100.9 1.4 fusion.26
  102.4 0.1 copy.47
  102.6 1.4 fusion.26
  104.1 0.1 copy.47
  104.3 1.4 fusion.26
  105.8 0.1 copy.47
  106.0 1.4 fusion.26
  107.5 0.1 copy.47
  107.7 1.4 fusion.26
  109.1 0.1 copy.22
  109.2 0.2 divide_convert_fusion
  109.4 2.5 %fusion.14 = f32[128,576]{0,1:T(8,128)} fusion(bf16[576,1024]{1,0:T(8,128)(2,1)} %param.12, bf16[16,8,8,128]{3,2,1,0:T(8,128)(2,1)S(1)} %bitcast.57), kind=kOutput, calls=%fused_computation.25 | convolution fusion | flops 150994944 | bytes 1736704 | tf_op jit(solution)/shard_map/dot_general | solution.py:59
  111.9 31.2 %all-reduce.2.cloned.1.call-done = f32[128,576]{0,1:T(8,128)} async-done(((f32[128,576]{0,1:T(8,128)}), f32[128,576]{0,1:T(8,128)}) %all-reduce.2.cloned.1.call-update) | async-done | bytes 294928 | tf_op jit(solution)/shard_map/psum | solution.py:62
  143.1 1.1 multiply_reduce_fusion
  144.2 21.4 %psum.15 = f32[128]{0:T(128)S(1)} all-reduce(f32[128]{0:T(128)S(1)} %multiply_reduce_fusion), channel_id=1, replica_groups=mesh['seq'=8,'head'=4] {'seq'}, use_global_device_ids=true, to_apply=%region_6.7 | all-reduce | flops 128 | bytes 1024 | tf_op jit(solution)/shard_map/psum | solution.py:64
  165.5 1.8 %multiply_convert_fusion = bf16[128,576]{0,1:T(8,128)(2,1)} fusion(f32[128,576]{0,1:T(8,128)} %all-reduce.2.cloned.1.call-done, f32[576]{0:T(1024)S(1)} %copy-done.2, f32[128]{0:T(128)S(1)} %add_rsqrt_fusion), kind=kLoop, calls=%fused_computation.23 | loop fusion | flops 221184 | bytes 445184 | tf_op jit(solution)/shard_map/convert_element_type | solution.py:67
  (29 shorter events, 0.8 us)
Async XLA Ops:
  6.5 4.7 %copy-start = (bf16[2048,4,128]{2,1,0:T(4,128)(2,1)S(1)}, bf16[2048,4,128]{2,1,0:T(4,128)(2,1)}, u32[]{:S(2)}) copy-start(bf16[2048,4,128]{2,1,0:T(4,128)(2,1)} %param.10) | copy-start | bytes 6291460
  6.5 85.7 %all-gather.2.cloned.1.call-start = ((), (), s32[]{:S(2)}) async-start(), calls=%async_computation | async-start | bytes 4718592 | tf_op jit(solution)/shard_map/all_gather | solution.py:11
  11.2 3.5 %copy-start.1 = (f32[4,2048,128,2]{2,1,3,0:T(8,128)}, f32[4,2048,128,2]{2,1,3,0:T(8,128)S(1)}, u32[]{:S(2)}) copy-start(f32[4,2048,128,2]{2,1,3,0:T(8,128)S(1)} %get-tuple-element.64) | copy-start | bytes 25165828
  15.9 127.2 %all-reduce.2.cloned.1.call-start = ((), (), s32[]{:S(2)}) async-start(), calls=%async_computation.1 | async-start | bytes 589824 | tf_op jit(solution)/shard_map/psum | solution.py:62
  93.3 72.2 %copy-start.2 = (f32[576]{0:T(1024)S(1)}, f32[576]{0:T(1024)}, u32[]{:S(2)}) copy-start(f32[576]{0:T(1024)} %param.13) | copy-start | bytes 6916
Sparse Core Ops, SparseCore 0:
  16.0 76.1 all-gather.1
  112.0 31.0 all-reduce.1
where the time goes:
time: 175 us; the launch traced here: 174 us
  blocking collectives  86.2 us (49%)
  waiting for transfers between devices  38.1 us (22%)
  other arithmetic  17.8 us (10%)
  between operations  14.3 us (8%)
  matrix products  9.75 us (6%)
  local copies, waits for them, and re-layouts  7.82 us (4%)
    all_gather x2, blocking collectives, merged(): pieces = jax.tree.map(lambda part: lax.all_gather(part, axis), value)  64.8 us
    psum x1, waiting for transfers between devices, body(): projected = lax.psum(projected_part, 'head')  31.2 us
    psum x1, blocking collectives, body(): square_total = lax.psum(square_part, 'seq')  21.4 us
    add x7, other arithmetic, combine_partials(): factor_former[..., None] * acc_former  10 us
    all_gather x1, waiting for transfers between devices, merged(): pieces = jax.tree.map(lambda part: lax.all_gather(part, axis), value)  6.87 us
    reduce_sum x1, other arithmetic, body(): block_sum = jnp.sum(weights, axis=-1)  4.59 us
    slice x3, local copies, waits for them, and re-layouts, merged(): tail = jax.tree.map(lambda part: part[1:], pieces)  4.08 us
    dot_general x1, matrix products, body(): jnp.einsum('tkgd,ckd->kgtc', grouped, key_cache, preferred_element_type=j...  3.86 us
  transfers between devices with their start and end apart: 2, of which 2 were waited for; matrix products, arithmetic and copies ran while one was open for 3% of the time, Pallas kernels for 0%

commit v1 on v0

--- a/solution.py
+++ b/solution.py
@@ -59,7 +59,8 @@
     projected_part = lax.dot_general(
         attention, out_weight, (((1,), (1,)), ((), ())), preferred_element_type=jnp.float32
     )
-    projected = lax.psum(projected_part, "head")
+    blocks = lax.all_gather(projected_part, "head")
+    projected = jnp.sum(blocks, axis=0)
     square_part = jnp.sum(projected * projected, axis=-1)
     square_total = lax.psum(square_part, "seq")
     mean_square = square_total / D

time: 175 us -> 163 us (0.931)
  waiting for transfers between devices: 38.1 us -> 23.2 us
    psum x1 -> x0, waiting for transfers between devices: 31.2 us -> none  [body(): projected = lax.psum(projected_part, 'head')]
    all_gather x0 -> x1, waiting for transfers between devices: none -> 16.3 us  [body(): blocks = lax.all_gather(projected_part, 'head')]
where the time goes in v1:
time: 163 us; the launch traced here: 162 us
  blocking collectives  86.2 us (53%)
  waiting for transfers between devices  23.2 us (14%)
  other arithmetic  19.2 us (12%)
  between operations  14.3 us (9%)
  matrix products  9.78 us (6%)
  local copies, waits for them, and re-layouts  9.47 us (6%)
    all_gather x2, blocking collectives, merged(): pieces = jax.tree.map(lambda part: lax.all_gather(part, axis), value)  64.8 us
    psum x1, blocking collectives, body(): square_total = lax.psum(square_part, 'seq')  21.4 us
    all_gather x1, waiting for transfers between devices, body(): blocks = lax.all_gather(projected_part, 'head')  16.3 us
    add x7, other arithmetic, combine_partials(): factor_former[..., None] * acc_former  10 us
    all_gather x1, waiting for transfers between devices, merged(): pieces = jax.tree.map(lambda part: lax.all_gather(part, axis), value)  6.87 us
    reduce_sum x1, other arithmetic, body(): block_sum = jnp.sum(weights, axis=-1)  4.59 us
    slice x3, local copies, waits for them, and re-layouts, merged(): tail = jax.tree.map(lambda part: part[1:], pieces)  4.08 us
    dot_general x1, matrix products, body(): jnp.einsum('tkgd,ckd->kgtc', grouped, key_cache, preferred_element_type=j...  3.86 us
  transfers between devices with their start and end apart: 2, of which 2 were waited for; matrix products, arithmetic and copies ran while one was open for 3% of the time, Pallas kernels for 0%

profile of v1, /device:TPU:0, one launch (start us, length us, event | category | flops | bytes accessed | tf_op | source)
XLA Modules:
  0.0 162.3 jit_solution(6585406153136113833)
XLA Ops:
  7.4 3.9 %bitcast_reduce_fusion = (f32[4,2,128]{2,1,0:T(2,128)S(1)}, f32[4,2048,128,2]{2,1,3,0:T(8,128)S(1)}) fusion(pred[2048]{0:T(1024)(128)(4,1)S(1)} %iota_compare_fusion, bf16[128,4,2,128]{3,2,1,0:T(2,128)(2,1)} %bitcast.64, bf16[2048,4,128,1]{2,1,0,3:T(4,128)(2,1)} %bitcast.63), kind=kOutput, calls=%fused_computation.9 | convolution fusion | flops 543161344 | bytes 10754048 | tf_op jit(solution)/shard_map/tkgd,ckd->kgtc/dot_general | solution.py:36
  11.2 3.4 %fusion.7 = f32[4,2,128,128]{3,2,1,0:T(8,128)S(1)} fusion(f32[4,2048,128,2]{2,1,3,0:T(8,128)S(1)} %get-tuple-element.64, f32[4,2,128]{2,1,0:T(2,128)S(1)} %get-tuple-element.63, pred[2048]{0:T(1024)(128)(4,1)S(1)} %iota_compare_fusion, bf16[2048,4,128,1]{2,1,0,3:T(4,128)(2,1)S(1)} %bitcast.58), kind=kOutput, calls=%fused_computation.15 | convolution fusion | flops 547356672 | bytes 11016192 | tf_op jit(solution)/shard_map/kgtc,ckd->tkgd/dot_general | solution.py:45
  14.7 1.1 copy.21
  15.9 4.6 %fusion.6 = f32[4,2,128]{2,1,0:T(2,128)S(1)} fusion(f32[4,2048,128,2]{2,1,3,0:T(8,128)} %copy-done.1, f32[4,2,128]{2,1,0:T(2,128)S(1)} %get-tuple-element.63, pred[2048]{0:T(1024)(128)(4,1)S(1)} %iota_compare_fusion), kind=kLoop, calls=%fused_computation.14 | loop fusion | flops 10484736 | bytes 8398848 | tf_op jit(solution)/shard_map/reduce_sum | solution.py:43
  20.5 33.0 %all_gather.16 = f32[8,128,8]{1,2,0:T(8,128)S(1)} all-gather(f32[1,128,8]{1,2,0:T(8,128)S(1)} %bitcast.62), channel_id=1, replica_groups=mesh['seq'=8,'head'=4] {'seq'}, dimensions={0}, use_global_device_ids=true | all-gather | bytes 36864 | tf_op jit(solution)/shard_map/all_gather | solution.py:11
  53.5 31.8 %all_gather.15 = f32[8,128,8]{1,2,0:T(8,128)S(1)} all-gather(f32[1,128,8]{1,2,0:T(8,128)S(1)} %bitcast.61), channel_id=1, replica_groups=mesh['seq'=8,'head'=4] {'seq'}, dimensions={0}, use_global_device_ids=true | all-gather | bytes 36864 | tf_op jit(solution)/shard_map/all_gather | solution.py:11
  85.3 6.9 %all-gather.4.cloned.1.call-done = f32[8,128,8,128]{3,2,1,0:T(8,128)} async-done(((f32[1,128,8,128]{3,2,1,0:T(8,128)}), f32[8,128,8,128]{3,2,1,0:T(8,128)}) %all-gather.4.cloned.1.call-update) | async-done | bytes 4194320 | tf_op jit(solution)/shard_map/all_gather | solution.py:11
  92.2 1.1 slice_bitcast_fusion
  93.3 4.1 %slice.29 = f32[7,128,8,128]{3,2,1,0:T(8,128)} slice(f32[8,128,8,128]{3,2,1,0:T(8,128)} %all-gather.4.cloned.1.call-done), slice={[1:8], [0:128], [0:8], [0:128]} | slice | bytes 7340032 | tf_op jit(solution)/shard_map/slice | solution.py:13
  97.4 11.7 %while.14 = (s32[]{:T(128)}, f32[128,8]{0,1:T(8,128)S(1)}, f32[128,8]{0,1:T(8,128)S(1)}, f32[128,8,128]{2,1,0:T(8,128)S(1)}, f32[7,128,8]{1,2,0:T(8,128)S(1)}, /...) while((s32[]{:T(128)}, f32[128,8]{0,1:T(8,128)S(1)}, f32[128,8]{0,1:T(8,128)S(1)}, ...), condition=%wide.region_3.4_spmd, body=%wide.region_2.3_spmd.sunk | while | flops 399362 | bytes 1630309 | solution.py:14
  97.4 0.1 copy.47
  97.6 1.4 fusion.26
  99.0 0.1 copy.47
  99.2 1.4 fusion.26
  100.7 0.1 copy.47
  100.9 1.4 fusion.26
  102.4 0.1 copy.47
  102.6 1.4 fusion.26
  104.1 0.1 copy.47
  104.3 1.4 fusion.26
  105.8 0.1 copy.47
  106.0 1.4 fusion.26
  107.4 0.1 copy.47
  107.6 1.4 fusion.26
  109.2 0.2 divide_convert_fusion
  109.4 2.5 %fusion.14 = f32[128,576]{0,1:T(8,128)} fusion(bf16[576,1024]{1,0:T(8,128)(2,1)} %param.12, bf16[16,8,8,128]{3,2,1,0:T(8,128)(2,1)S(1)} %bitcast.59), kind=kOutput, calls=%fused_computation.25 | convolution fusion | flops 150994944 | bytes 1736704 | tf_op jit(solution)/shard_map/dot_general | solution.py:59
  111.9 16.3 %all-gather.6.cloned.1.call-done = f32[512,576]{0,1:T(8,128)} async-done(((f32[128,576]{0,1:T(8,128)}), f32[512,576]{0,1:T(8,128)}) %all-gather.6.cloned.1.call-update) | async-done | bytes 1179664 | tf_op jit(solution)/shard_map/all_gather | solution.py:62
  128.2 1.7 %reshape.12 = f32[4,128,576]{1,0,2:T(4,128)S(1)} reshape(f32[512,576]{0,1:T(8,128)} %all-gather.6.cloned.1.call-done) | data formatting | bytes 2359296 | tf_op jit(solution)/shard_map/all_gather | solution.py:62
  129.8 1.4 reduce_sum.28
  131.3 1.1 multiply_reduce_fusion
  132.3 21.4 %psum.7 = f32[128]{0:T(128)S(1)} all-reduce(f32[128]{0:T(128)S(1)} %multiply_reduce_fusion), channel_id=1, replica_groups=mesh['seq'=8,'head'=4] {'seq'}, use_global_device_ids=true, to_apply=%region_6.7 | all-reduce | flops 128 | bytes 1024 | tf_op jit(solution)/shard_map/psum | solution.py:65
  153.7 1.8 %multiply_convert_fusion = bf16[128,576]{0,1:T(8,128)(2,1)} fusion(f32[128,576]{0,1:T(8,128)} %reduce_sum.28, f32[576]{0:T(1024)S(1)} %copy-done.2, f32[128]{0:T(128)S(1)} %add_rsqrt_fusion), kind=kLoop, calls=%fused_computation.23 | loop fusion | flops 221184 | bytes 445184 | tf_op jit(solution)/shard_map/convert_element_type | solution.py:68
  (31 shorter events, 1.0 us)
Async XLA Ops:
  6.5 4.7 %copy-start = (bf16[2048,4,128]{2,1,0:T(4,128)(2,1)S(1)}, bf16[2048,4,128]{2,1,0:T(4,128)(2,1)}, u32[]{:S(2)}) copy-start(bf16[2048,4,128]{2,1,0:T(4,128)(2,1)} %param.10) | copy-start | bytes 6291460
  6.5 85.7 %all-gather.4.cloned.1.call-start = ((), (), s32[]{:S(2)}) async-start(), calls=%async_computation | async-start | bytes 4718592 | tf_op jit(solution)/shard_map/all_gather | solution.py:11
  11.2 3.5 %copy-start.1 = (f32[4,2048,128,2]{2,1,3,0:T(8,128)}, f32[4,2048,128,2]{2,1,3,0:T(8,128)S(1)}, u32[]{:S(2)}) copy-start(f32[4,2048,128,2]{2,1,3,0:T(8,128)S(1)} %get-tuple-element.64) | copy-start | bytes 25165828
  15.9 112.3 %all-gather.6.cloned.1.call-start = ((), (), s32[]{:S(2)}) async-start(), calls=%async_computation.1 | async-start | bytes 1474560 | tf_op jit(solution)/shard_map/all_gather | solution.py:62
  97.4 56.4 %copy-start.2 = (f32[576]{0:T(1024)S(1)}, f32[576]{0:T(1024)}, u32[]{:S(2)}) copy-start(f32[576]{0:T(1024)} %param.13) | copy-start | bytes 6916
Sparse Core Ops, SparseCore 0:
  16.0 76.1 all-gather.3
  112.0 16.1 all-gather.5
